TPU v7x, 512 devices: a whole 4x8x8 slice. The times are simulated.
512 devices in a mesh: chan: 16 (over x_hi, z), tm: 8 (over y), row: 4 (over x_lo, core).
Axes of the slice: x: 4 (x_hi: 2, x_lo: 2; x = x_hi * 2 + x_lo), y: 8, z: 8, core: 2. Of those that a mesh axis runs over, the one named last changes fastest.
Arguments:
- samples: bfloat16 [32, 4096, 4096], P(('tm', 'row'), None, 'chan'), may hold values from -6 to 6
- channel_index: int32 [16], replicated, may hold values from 1 to 2047
- gain_real: float32 [16, 4096], P(None, 'chan'), may hold values from -4 to 4
- gain_imag: float32 [16, 4096], P(None, 'chan'), may hold values from -4 to 4
- flags: int32 [2048], P('chan'), may hold values 0 or 1
Outputs:
- visibility: bfloat16 [2, 16, 4096, 4096], P(None, 'chan', 'row', 'tm')
Inputs may be any that keep to these rules, and one draw needn't show every extreme that they name: `channel_index`: channel numbers, not necessarily distinct.
All inputs are finite; a program needn't handle non-finite values. No bound on the sum of `flags` on one device may be relied on, other than what follows from the above.
Results may differ from a plain program's by a relative error of at most 0.0056.
Values may be sent and summed in bfloat16 or wider, within the bound.
A program may use at most 64 MiB of HBM per device.

v0:
```python
import math

import jax
import jax.numpy as jnp
from jax import lax
from jax.sharding import PartitionSpec as P

P_SIZE = 4096
TAPS = 4
CHANNELS = 16


def shifted(value, axis, by):
    peers = lax.axis_size(axis)
    pairs = [(i, i + by) for i in range(peers) if 0 <= i + by < peers]
    return lax.ppermute(value, axis, pairs)


def laid_out(tiles, dim):
    dims = list(tiles.shape[1:])
    dims[dim] *= tiles.shape[0]
    return jnp.moveaxis(tiles, 0, dim).reshape(dims)


def from_everyone(value, axis):
    copies = jnp.broadcast_to(value, (lax.axis_size(axis), *value.shape))
    return lax.all_to_all(copies, axis, split_axis=0, concat_axis=0, tiled=True)


def collect(value, axis, dim):
    return laid_out(from_everyone(value, axis), dim)


def filter_taps():
    sample_index = jnp.arange(TAPS * P_SIZE, dtype=jnp.int32).astype(jnp.float32)
    centered = (sample_index + 0.5 - TAPS * P_SIZE / 2) / P_SIZE
    hann_taper = 0.5 - 0.5 * jnp.cos(2.0 * math.pi * (sample_index + 0.5) / (TAPS * P_SIZE))
    return (jnp.sinc(centered) * hann_taper).reshape(TAPS, P_SIZE)


def dft_table(channel_index):
    points = jnp.arange(P_SIZE, dtype=jnp.int32)
    phase_index = channel_index[:, None] * points[None, :] % P_SIZE
    angles = 2.0 * math.pi * phase_index.astype(jnp.float32) / P_SIZE
    scale = 1.0 / math.sqrt(P_SIZE)
    return jnp.concatenate([jnp.cos(angles) * scale, -jnp.sin(angles) * scale], 0)


def local(samples, channel_index, gain_real, gain_imag, flags):
    frames_dev = samples.shape[0]
    filters = filter_taps()
    table = dft_table(channel_index)
    shifts_needed = (TAPS - 2) // frames_dev + 1
    tables = filters[:, None, :] * table[None]
    partials = jnp.einsum(
        "kcp,fpi->kfci", tables, samples.astype(jnp.float32), precision=lax.Precision.HIGHEST
    )
    length = (shifts_needed + 1) * frames_dev
    local_sum = None
    for tap_number in range(TAPS):
        before = TAPS - 1 - tap_number
        placed = jnp.pad(
            partials[tap_number], ((before, length - frames_dev - before), (0, 0), (0, 0))
        )
        local_sum = placed if local_sum is None else local_sum + placed
    spectra = local_sum[0:frames_dev]
    for offset in range(1, shifts_needed + 1):
        spectra = spectra + shifted(
            local_sum[offset * frames_dev : (offset + 1) * frames_dev], ("tm", "row"), offset
        )
    spec_re = spectra[:, :CHANNELS]
    spec_im = spectra[:, CHANNELS:]
    usable = jnp.repeat(flags, 2).astype(jnp.float32)
    volt_re = (usable * (gain_real * spec_re - gain_imag * spec_im)).astype(jnp.bfloat16)
    volt_im = (usable * (gain_real * spec_im + gain_imag * spec_re)).astype(jnp.bfloat16)
    turned = jnp.stack([volt_re, volt_im], 1)
    turned = lax.all_to_all(turned, "chan", split_axis=2, concat_axis=3, tiled=True)
    inputs_total = turned.shape[3]
    row_count = inputs_total // lax.axis_size("row")
    col_count = inputs_total // lax.axis_size("tm")
    whole_panel = collect(turned, ("tm", "row"), 0)
    frames_total = whole_panel.shape[0]
    row_start = lax.axis_index("row") * row_count
    col_start = lax.axis_index("tm") * col_count
    panel_re = whole_panel[:, 0]
    panel_im = whole_panel[:, 1]
    rows_re = lax.dynamic_slice_in_dim(panel_re, row_start, row_count, 2)
    rows_im = lax.dynamic_slice_in_dim(panel_im, row_start, row_count, 2)
    cols_re = lax.dynamic_slice_in_dim(panel_re, col_start, col_count, 2)
    cols_im = lax.dynamic_slice_in_dim(panel_im, col_start, col_count, 2)
    left_side = jnp.concatenate([rows_re, rows_im], 0)
    right_side = jnp.concatenate(
        [jnp.concatenate([cols_re, -cols_im], 2), jnp.concatenate([cols_im, cols_re], 2)], 0
    )
    product = jnp.einsum("fcr,fcq->crq", left_side, right_side, preferred_element_type=jnp.float32)
    result = jnp.stack([product[:, :, :col_count], product[:, :, col_count:]], 0) / frames_total
    return result.astype(jnp.bfloat16)


def solution(mesh):
    in_specs = (P(("tm", "row"), None, "chan"), P(), P(None, "chan"), P(None, "chan"), P("chan"))
    out_specs = P(None, "chan", "row", "tm")
    return jax.shard_map(local, mesh=mesh, in_specs=in_specs, out_specs=out_specs, check_vma=False)
```

profile of v0, /device:TPU:1, one launch (start us, length us, event | category | flops | bytes accessed | tf_op | source)
XLA Modules:
  0.0 70.3 jit_solution(7527728988987634632)
XLA Ops:
  0.0 0.0 copy-start
  0.0 0.6 fusion.25
  0.6 1.8 %cosine_multiply_fusion = (f32[16,4096]{1,0:T(8,128)S(1)}, f32[16,4096]{1,0:T(8,128)S(1)}) fusion(s32[16]{0:T(128)} %param.6), kind=kLoop, calls=%fused_computation.19 | loop fusion | flops 1114112 | bytes 524352 | tf_op jit(solution)/shard_map/mul | solution.py:46
  2.4 0.0 copy-start.3
  2.5 0.0 copy-start.1
  2.5 0.0 copy-start.2
  2.5 1.2 %fusion.1 = f32[4,32,256]{2,1,0:T(8,128)S(1)} fusion(bf16[1,4096,256]{2,1,0:T(8,128)(2,1)S(1)} %copy-done, f32[32,4096]{1,0:T(8,128)S(1)} %pad_maximum_fusion, f32[4,4096]{1,0:T(4,128)S(1)} %fusion.25), kind=kOutput, calls=%fused_computation.5 | convolution fusion | flops 1611137024 | bytes 2818048 | tf_op jit(solution)/shard_map/kcp,fpi->kfci/dot_general | solution.py:55
  3.8 4.5 %collective-permute-start = (f32[1,32,256]{2,1,0:T(8,128)S(1)}, f32[1,32,256]{2,1,0:T(8,128)S(1)}, u32[]{:S(2)}, u32[]{:S(2)}) collective-permute-start(f32[1,32,256]{2,1,0:T(8,128)S(1)} %get-tuple-element.11), channel_id=1, source_target_pairs={{0,1},{1,2},{2,3},{3,4},{4,5},{5,6},{6,7},{7,8},{8,9},{9,10},{10,1... | collective-permute-start | bytes 98312 | tf_op jit(solution)/shard_map/ppermute | solution.py:16
  8.3 2.0 %collective-permute-start.2 = (f32[1,32,256]{2,1,0:T(8,128)S(1)}, f32[1,32,256]{2,1,0:T(8,128)S(1)}, u32[]{:S(2)}, u32[]{:S(2)}) collective-permute-start(f32[1,32,256]{2,1,0:T(8,128)S(1)} %get-tuple-element.12), channel_id=1, source_target_pairs={{0,3},{1,4},{2,5},{3,6},{4,7},{5,8},{6,9},{7,10},{8,11},{9,12},{10... | collective-permute-start | bytes 98312 | tf_op jit(solution)/shard_map/ppermute | solution.py:16
  10.3 3.1 %collective-permute-start.1 = (f32[1,32,256]{2,1,0:T(8,128)S(1)}, f32[1,32,256]{2,1,0:T(8,128)S(1)}, u32[]{:S(2)}, u32[]{:S(2)}) collective-permute-start(f32[1,32,256]{2,1,0:T(8,128)S(1)} %get-tuple-element.13), channel_id=1, source_target_pairs={{0,2},{1,3},{2,4},{3,5},{4,6},{5,7},{6,8},{7,9},{8,10},{9,11},{10,... | collective-permute-start | bytes 98312 | tf_op jit(solution)/shard_map/ppermute | solution.py:16
  13.4 0.0 copy-done.3
  13.4 0.1 broadcast_in_dim.24
  13.5 0.1 convert_element_type.53
  13.7 0.0 collective-permute-done
  13.7 0.0 collective-permute-done.2
  13.7 0.9 %collective-permute-done.1 = f32[1,32,256]{2,1,0:T(8,128)S(1)} collective-permute-done((f32[1,32,256]{2,1,0:T(8,128)S(1)}, f32[1,32,256]{2,1,0:T(8,128)S(1)}, u32[]{:S(2)}, u32[]{:S(2)}) %collective-permute-start.1) | collective-permute-done | bytes 32800 | tf_op jit(solution)/shard_map/ppermute | solution.py:16
  14.7 21.0 %all_to_all.17 = bf16[1,2,16,256]{3,1,0,2:T(2,128)(2,1)S(1)} all-to-all(bf16[1,2,16,256]{3,1,0,2:T(2,128)(2,1)S(1)} %copy.20), channel_id=1, replica_groups=mesh['chan'=16,'tm'=8,'row'=4] {'chan'}, dimensions={2} | all-to-all | bytes 32768 | tf_op jit(solution)/shard_map/all_to_all | solution.py:77
  35.7 1.3 %broadcast_in_dim.27 = bf16[32,1,2,1,4096]{4,2,3,1,0:T(2,128)(2,1)} broadcast(bf16[2,4096]{1,0:T(2,128)(2,1)S(1)} %bitcast.83), dimensions={2,4} | broadcast | bytes 540672 | tf_op jit(solution)/shard_map/broadcast_in_dim | solution.py:26
  37.0 13.2 %all-to-all-start.1 = ((bf16[32,1,2,1,4096]{4,2,3,1,0:T(2,128)(2,1)}), bf16[32,1,2,1,4096]{4,2,3,1,0:T(2,128)(2,1)S(1)}, u32[]{:S(2)}, u32[]{:S(2)}) async-start(bf16[32,1,2,1,4096]{4,2,3,1,0:T(2,128)(2,1)} %broadcast_in_dim.27), calls=%async_computation.1 | async-start | bytes 1048576 | tf_op jit(solution)/shard_map/all_to_all | solution.py:27
  50.2 16.6 %all-to-all-done.1 = bf16[32,1,2,1,4096]{4,2,3,1,0:T(2,128)(2,1)S(1)} async-done(((bf16[32,1,2,1,4096]{4,2,3,1,0:T(2,128)(2,1)}), bf16[32,1,2,1,4096]{4,2,3,1,0:T(2,128)(2,1)S(1)}, u32[]{:S(2)}, u32[]{:S(2)}) %all-to-all-start.1) | async-done | bytes 524320 | tf_op jit(solution)/shard_map/all_to_all | solution.py:27
  66.7 0.3 copy.23
  67.1 0.7 %convolution_bitcast_fusion = f32[1,1024,1024]{2,1,0:T(8,128)S(1)} fusion(bf16[32,1,1024]{2,0,1:T(8,128)(2,1)S(1)} %get-tuple-element.21, bf16[32,1,1024]{2,0,1:T(8,128)(2,1)S(1)} %get-tuple-element.22, bf16[32,1,512]{2,0,1:T(8,128)(2,1)S(1)} %dynamic-slice_bitcast_fusion.3, bf16[32,1,512]{2,0,1:T(8,128)(2,1)S(1)} %get-tuple-element.6, ...), kind=kOutput, calls=%fused_computation.2 | convolution fusion | flops 135004160 | bytes 4423680 | tf_op jit(solution)/shard_map/fcr,fcq->crq/dot_general | solution.py:95
  67.9 0.5 slice_bitcast_fusion.1
  68.4 1.9 %fusion = bf16[2,1,1024,512]{3,2,1,0:T(8,128)(2,1)} fusion(f32[1,1,1024,512]{3,2,1,0:T(8,128)S(1)} %get-tuple-element.8, f32[1,1,1024,512]{3,2,1,0:T(8,128)S(1)} %get-tuple-element.7), kind=kLoop, calls=%fused_computation.1 | loop fusion | flops 3145728 | bytes 6291456 | tf_op jit(solution)/shard_map/convert_element_type | solution.py:97
  (17 shorter events, 0.2 us)
Async XLA Ops:
  0.0 2.5 %copy-start = (bf16[1,4096,256]{2,1,0:T(8,128)(2,1)S(1)}, bf16[1,4096,256]{2,1,0:T(8,128)(2,1)}, u32[]{:S(2)}) copy-start(bf16[1,4096,256]{2,1,0:T(8,128)(2,1)} %param.5) | copy-start | bytes 6291460
  2.4 11.0 %copy-start.3 = (s32[128]{0:T(128)S(1)}, s32[128]{0:T(128)}, u32[]{:S(2)}) copy-start(s32[128]{0:T(128)} %param.9) | copy-start | bytes 1540
  2.5 12.1 %copy-start.1 = (f32[16,256]{1,0:T(8,128)S(1)}, f32[16,256]{1,0:T(8,128)}, u32[]{:S(2)}) copy-start(f32[16,256]{1,0:T(8,128)} %param.8) | copy-start | bytes 49156
  2.5 12.1 %copy-start.2 = (f32[16,256]{1,0:T(8,128)S(1)}, f32[16,256]{1,0:T(8,128)}, u32[]{:S(2)}) copy-start(f32[16,256]{1,0:T(8,128)} %param.7) | copy-start | bytes 49156
  3.8 9.9 %collective-permute-start = (f32[1,32,256]{2,1,0:T(8,128)S(1)}, f32[1,32,256]{2,1,0:T(8,128)S(1)}, u32[]{:S(2)}, u32[]{:S(2)}) collective-permute-start(f32[1,32,256]{2,1,0:T(8,128)S(1)} %get-tuple-element.11), channel_id=1, source_target_pairs={{0,1},{1,2},{2,3},{3,4},{4,5},{5,6},{6,7},{7,8},{8,9},{9,10},{10,1... | collective-permute-start | bytes 98312 | tf_op jit(solution)/shard_map/ppermute | solution.py:16
  8.3 5.4 %collective-permute-start.2 = (f32[1,32,256]{2,1,0:T(8,128)S(1)}, f32[1,32,256]{2,1,0:T(8,128)S(1)}, u32[]{:S(2)}, u32[]{:S(2)}) collective-permute-start(f32[1,32,256]{2,1,0:T(8,128)S(1)} %get-tuple-element.12), channel_id=1, source_target_pairs={{0,3},{1,4},{2,5},{3,6},{4,7},{5,8},{6,9},{7,10},{8,11},{9,12},{10... | collective-permute-start | bytes 98312 | tf_op jit(solution)/shard_map/ppermute | solution.py:16
  10.3 4.3 %collective-permute-start.1 = (f32[1,32,256]{2,1,0:T(8,128)S(1)}, f32[1,32,256]{2,1,0:T(8,128)S(1)}, u32[]{:S(2)}, u32[]{:S(2)}) collective-permute-start(f32[1,32,256]{2,1,0:T(8,128)S(1)} %get-tuple-element.13), channel_id=1, source_target_pairs={{0,2},{1,3},{2,4},{3,5},{4,6},{5,7},{6,8},{7,9},{8,10},{9,11},{10,... | collective-permute-start | bytes 98312 | tf_op jit(solution)/shard_map/ppermute | solution.py:16
  37.0 29.7 %all-to-all-start.1 = ((bf16[32,1,2,1,4096]{4,2,3,1,0:T(2,128)(2,1)}), bf16[32,1,2,1,4096]{4,2,3,1,0:T(2,128)(2,1)S(1)}, u32[]{:S(2)}, u32[]{:S(2)}) async-start(bf16[32,1,2,1,4096]{4,2,3,1,0:T(2,128)(2,1)} %broadcast_in_dim.27), calls=%async_computation.1 | async-start | bytes 1048576 | tf_op jit(solution)/shard_map/all_to_all | solution.py:27
where the time goes:
time: 70.8 us; the launch traced here: 70.3 us
  starting transfers between devices  22.8 us (32%)
  blocking collectives  21 us (30%)
  waiting for transfers between devices  17.5 us (25%)
  other arithmetic  4.41 us (6%)
  local copies, waits for them, and re-layouts  2.45 us (3%)
  matrix products  1.9 us (3%)
    all_to_all x1, blocking collectives, local(): lax.all_to_all(turned, 'chan', split_axis=2, concat_axis=3, tiled=True)  21 us
    all_to_all x1, waiting for transfers between devices, from_everyone(): return lax.all_to_all(copies, axis, split_axis=0, concat_axis=0, tiled=True)  16.6 us
    all_to_all x1, starting transfers between devices, from_everyone(): return lax.all_to_all(copies, axis, split_axis=0, concat_axis=0, tiled=True)  13.2 us
    ppermute x3, starting transfers between devices, shifted(): return lax.ppermute(value, axis, pairs)  9.62 us
    convert_element_type x1, other arithmetic, local(): return result.astype(jnp.bfloat16)  1.89 us
    mul x1, other arithmetic, dft_table(): jnp.cos(angles) * scale  1.8 us
  transfers between devices with their start and end apart: 4, of which 2 were waited for; matrix products, arithmetic and copies ran while one was open for 0% of the time, Pallas kernels for 0%

commit v1 on v0

v1 whole, which is shorter than its diff:
```python
import functools
import math

import jax
import jax.numpy as jnp
import numpy as np
from jax import lax
from jax.experimental import pallas as pl
from jax.experimental.pallas import tpu as pltpu
from jax.sharding import PartitionSpec as P

P_SIZE = 4096
TAPS = 4
CHANNELS = 16
N_CHAN, N_TM, N_ROW = 16, 8, 4
N_FRAMES = N_TM * N_ROW
BLOCK = 256
CHUNK = 512
MESH = pl.DeviceIdType.MESH
F32, BF16 = jnp.float32, jnp.bfloat16


def filter_taps():
    at = np.arange(TAPS * P_SIZE, dtype=np.float64) + 0.5
    centered = (at - TAPS * P_SIZE / 2) / P_SIZE
    taper = 0.5 - 0.5 * np.cos(2.0 * math.pi * at / (TAPS * P_SIZE))
    return (np.sinc(centered) * taper).reshape(TAPS, P_SIZE).astype(np.float32)


def cos_sin(phase):
    quarter = lax.shift_right_logical(phase + 512, 10)
    rest = phase - lax.shift_left(quarter, 10)
    x = rest.astype(F32) * (2.0 * math.pi / P_SIZE)
    y = x * x
    s = x + x * y * (-1 / 6 + y * (1 / 120 + y * (-1 / 5040 + y * (1 / 362880))))
    c = 1.0 + y * (-0.5 + y * (1 / 24 + y * (-1 / 720 + y * (1 / 40320))))
    odd = (quarter & 1) == 1
    cos = jnp.where(odd, s, c)
    sin = jnp.where(odd, c, s)
    cos = jnp.where(((quarter + 1) & 2) == 2, -cos, cos)
    sin = jnp.where((quarter & 2) == 2, -sin, sin)
    return cos, sin


def far_first(i):
    half = (i + 1) // 2
    return 4 + half * (1 - 2 * (i % 2))


def gather_kernel(
    x_hbm, ci_hbm, filt_hbm, gr_hbm, gi_hbm, flags_hbm,
    rows_out, cols_out,
    x, ci, filt, gr, gi, flags, lhs, send, parts, volts,
    local_sems, send_sem1, send_sem2, parts_sems, rows_sem, cols_sem,
):
    me_c = lax.axis_index("chan")
    me_t = lax.axis_index("tm")
    me_r = lax.axis_index("row")
    frame = me_t * N_ROW + me_r

    loads = [
        pltpu.make_async_copy(src, dst, local_sems.at[i])
        for i, (src, dst) in enumerate(
            [(ci_hbm, ci), (filt_hbm, filt), (gr_hbm, gr), (gi_hbm, gi),
             (flags_hbm, flags), (x_hbm.at[0], x)]
        )
    ]
    for copy in loads:
        copy.start()

    barrier = pltpu.get_barrier_semaphore()

    def greet_chan(i, _):
        peer = (me_c + i) % N_CHAN
        for back in range(TAPS):
            @pl.when(frame >= back)
            def _():
                other = frame - back
                pl.semaphore_signal(
                    barrier, inc=1,
                    device_id=(peer, other // N_ROW, other % N_ROW), device_id_type=MESH,
                )
        return 0

    lax.fori_loop(1, N_CHAN, greet_chan, 0)

    def greet_frames(i, _):
        other = (frame + i) % N_FRAMES
        pl.semaphore_signal(
            barrier, inc=1,
            device_id=(me_c, other // N_ROW, other % N_ROW), device_id_type=MESH,
        )
        return 0

    lax.fori_loop(1, N_FRAMES, greet_frames, 0)

    for before in range(1, TAPS):
        @pl.when(frame < before)
        def _():
            parts[TAPS - 1 - before] = jnp.zeros(parts.shape[1:], F32)

    loads[0].wait()
    loads[1].wait()
    row_of = lax.broadcasted_iota(jnp.int32, (CHANNELS, CHUNK), 0)
    chan_at = jnp.zeros((CHANNELS, CHUNK), jnp.int32)
    for c in range(CHANNELS):
        chan_at = jnp.where(row_of == c, ci[c], chan_at)
    lane = lax.broadcasted_iota(jnp.int32, (CHANNELS, CHUNK), 1)

    def one_chunk(n, _):
        at = pl.ds(pl.multiple_of(n * CHUNK, CHUNK), CHUNK)
        phase = (chan_at * (lane + n * CHUNK)) & (P_SIZE - 1)
        cos, sin = cos_sin(phase)
        scale = 1.0 / math.sqrt(P_SIZE)
        table = (cos * scale, sin * -scale)
        for k in range(TAPS):
            tap = filt[k : k + 1, at]
            for part in range(2):
                value = table[part] * tap
                high = value.astype(BF16)
                low = (value - high.astype(F32)).astype(BF16)
                row = (2 * k + part) * CHANNELS
                lhs[row : row + CHANNELS, at] = high
                lhs[row + 128 : row + 128 + CHANNELS, at] = low
        return 0

    lax.fori_loop(0, P_SIZE // CHUNK, one_chunk, 0)

    for copy in loads[2:]:
        copy.wait()
    both = jnp.dot(lhs[...], x[...], preferred_element_type=F32)
    spectra = both[:128] + both[128:]

    twice = (
        lax.broadcasted_iota(jnp.int32, (128, BLOCK), 1) // 2
        == lax.broadcasted_iota(jnp.int32, (128, BLOCK), 0)
    ).astype(BF16)
    alive = jnp.dot(
        jnp.broadcast_to(flags[...].astype(F32), (CHANNELS, 128)).astype(BF16), twice,
        preferred_element_type=F32,
    )
    real_gain = gr[...] * alive
    imag_gain = gi[...] * alive
    planes = []
    for k in range(TAPS):
        s_re = spectra[32 * k : 32 * k + 16]
        s_im = spectra[32 * k + 16 : 32 * k + 32]
        planes += [real_gain * s_re - imag_gain * s_im, real_gain * s_im + imag_gain * s_re]
    planes = jnp.concatenate(planes, 0)
    to = lax.broadcasted_iota(jnp.int32, (128, 128), 0)
    source = (to % 8) * 16 + to // 8
    turn = (lax.broadcasted_iota(jnp.int32, (128, 128), 1) == source).astype(F32)
    turned = jnp.dot(
        turn, planes, precision=lax.Precision.HIGHEST, preferred_element_type=F32
    )
    send[...] = turned.reshape(64, 2, BLOCK)

    ahead_count = jnp.minimum(N_FRAMES - 1 - frame, TAPS - 1)
    pl.semaphore_wait(barrier, (N_CHAN - 1) * (1 + ahead_count) + N_FRAMES - 1)

    def part_copy(c, ahead):
        k = TAPS - 1 - ahead
        other = frame + ahead
        return pltpu.make_async_remote_copy(
            src_ref=send.at[c * TAPS + k],
            dst_ref=parts.at[k, me_c],
            send_sem=send_sem1.at[k],
            recv_sem=parts_sems.at[k],
            device_id=(c, other // N_ROW, other % N_ROW),
            device_id_type=MESH,
        )

    def send_parts(i, _):
        z = (me_c % 8 + far_first(i % 8)) % 8
        half = (me_c // 8 + 1 + i // 8) % 2
        c = half * 8 + z
        for ahead in range(TAPS - 1, 0, -1):
            @pl.when(frame + ahead < N_FRAMES)
            def _():
                part_copy(c, ahead).start()

        @pl.when(i < N_CHAN - 1)
        def _():
            part_copy(c, 0).start()
        return 0

    parts[TAPS - 1, me_c] = send[me_c * TAPS + TAPS - 1]
    lax.fori_loop(0, N_CHAN, send_parts, 0)

    for k in range(TAPS - 1):
        @pl.when(frame >= TAPS - 1 - k)
        def _():
            pltpu.make_async_copy(parts.at[k], parts.at[k], parts_sems.at[k]).wait()
    own = parts.at[TAPS - 1, pl.ds(0, N_CHAN - 1)]
    pltpu.make_async_copy(own, own, parts_sems.at[TAPS - 1]).wait()

    volts[...] = (((parts[0] + parts[1]) + parts[2]) + parts[3]).astype(BF16)

    def volt_copies(t, r):
        rows = pltpu.make_async_remote_copy(
            src_ref=volts.at[pl.ds(r * 4, 4)],
            dst_ref=rows_out.at[frame],
            send_sem=send_sem2.at[0],
            recv_sem=rows_sem,
            device_id=(me_c, t, r),
            device_id_type=MESH,
        )
        cols = pltpu.make_async_remote_copy(
            src_ref=volts.at[pl.ds(t * 2, 2)],
            dst_ref=cols_out.at[frame],
            send_sem=send_sem2.at[1],
            recv_sem=cols_sem,
            device_id=(me_c, t, r),
            device_id_type=MESH,
        )
        return rows, cols

    def send_volts(i, _):
        t = (me_t + far_first(i // 4)) % N_TM
        r = (me_r + 1 + i % 4) % N_ROW
        rows, cols = volt_copies(t, r)
        rows.start()
        cols.start()
        return 0

    rows_out[frame] = volts[pl.ds(me_r * 4, 4)]
    cols_out[frame] = volts[pl.ds(me_t * 2, 2)]
    lax.fori_loop(0, N_FRAMES - 1, send_volts, 0)

    for ref, sem in ((rows_out, rows_sem), (cols_out, cols_sem)):
        others = ref.at[pl.ds(0, N_FRAMES - 1)]
        pltpu.make_async_copy(others, others, sem).wait()

    for k in range(TAPS - 1):
        @pl.when(frame + TAPS - 1 - k < N_FRAMES)
        def _():
            pltpu.make_async_copy(parts.at[k], parts.at[k], send_sem1.at[k]).wait()
    pltpu.make_async_copy(own, own, send_sem1.at[TAPS - 1]).wait()
    for ref, at in ((rows_out, 0), (cols_out, 1)):
        others = ref.at[pl.ds(0, N_FRAMES - 1)]
        pltpu.make_async_copy(others, others, send_sem2.at[at]).wait()


def correlate_kernel(rows, cols, out, right):
    @pl.when(pl.program_id(0) == 0)
    def _():
        to = lax.broadcasted_iota(jnp.int32, (64, 64), 0)
        at = lax.broadcasted_iota(jnp.int32, (64, 64), 1)
        sign = jnp.where(to % 2 == 0, -1.0, 1.0)
        swap = jnp.where(at == to + 1 - 2 * (to % 2), sign, 0.0).astype(BF16)
        panel = jnp.concatenate([cols[:, 0].reshape(64, BLOCK), cols[:, 1].reshape(64, BLOCK)], 1)
        right[:, :512] = panel
        right[:, 512:] = jnp.dot(swap, panel, preferred_element_type=F32).astype(BF16)

    left = rows[:, pl.program_id(0)].reshape(64, BLOCK)
    product = lax.dot_general(
        left, right[...], (((0,), (0,)), ((), ())), preferred_element_type=F32
    )
    product = product * (1.0 / N_FRAMES)
    out[0, 0] = product[:, :512].astype(BF16)
    out[1, 0] = product[:, 512:].astype(BF16)


def local(samples, channel_index, gain_real, gain_imag, flags):
    anywhere = pl.BlockSpec(memory_space=pl.ANY)
    vmem = pl.BlockSpec(memory_space=pltpu.VMEM)
    rows, cols = pl.pallas_call(
        gather_kernel,
        out_shape=(
            jax.ShapeDtypeStruct((N_FRAMES, 4, 2, BLOCK), BF16),
            jax.ShapeDtypeStruct((N_FRAMES, 2, 2, BLOCK), BF16),
        ),
        in_specs=[anywhere] * 6,
        out_specs=(vmem, vmem),
        scratch_shapes=[
            pltpu.VMEM((P_SIZE, BLOCK), BF16),
            pltpu.SMEM((CHANNELS,), jnp.int32),
            pltpu.VMEM((TAPS, P_SIZE), F32),
            pltpu.VMEM((CHANNELS, BLOCK), F32),
            pltpu.VMEM((CHANNELS, BLOCK), F32),
            pltpu.VMEM((1, 128), jnp.int32),
            pltpu.VMEM((256, P_SIZE), BF16),
            pltpu.VMEM((CHANNELS * TAPS, 2, BLOCK), F32),
            pltpu.VMEM((TAPS, N_CHAN, 2, BLOCK), F32),
            pltpu.VMEM((N_CHAN, 2, BLOCK), BF16),
            pltpu.SemaphoreType.DMA((6,)),
            pltpu.SemaphoreType.DMA((TAPS,)),
            pltpu.SemaphoreType.DMA((2,)),
            pltpu.SemaphoreType.DMA((TAPS,)),
            pltpu.SemaphoreType.DMA,
            pltpu.SemaphoreType.DMA,
        ],
        compiler_params=pltpu.CompilerParams(
            collective_id=0, has_side_effects=True, vmem_limit_bytes=16 * 2**20
        ),
        name="spectra_and_gather",
    )(samples, channel_index, jnp.asarray(filter_taps()), gain_real, gain_imag,
      flags.reshape(1, 128))
    return pl.pallas_call(
        correlate_kernel,
        grid=(4,),
        out_shape=jax.ShapeDtypeStruct((2, 1, 1024, 512), BF16),
        in_specs=[vmem, vmem],
        out_specs=pl.BlockSpec((2, 1, BLOCK, 512), lambda i: (0, 0, i, 0)),
        scratch_shapes=[pltpu.VMEM((64, 1024), BF16)],
        compiler_params=pltpu.CompilerParams(vmem_limit_bytes=16 * 2**20),
        name="correlate",
    )(rows, cols)


def solution(mesh):
    in_specs = (P(("tm", "row"), None, "chan"), P(), P(None, "chan"), P(None, "chan"), P("chan"))
    out_specs = P(None, "chan", "row", "tm")
    return jax.shard_map(local, mesh=mesh, in_specs=in_specs, out_specs=out_specs, check_vma=False)
```

time: 70.8 us -> 39.1 us (0.55)
  Pallas kernels: 0 us -> 33.6 us
  starting transfers between devices: 22.8 us -> 0 us
  blocking collectives: 21 us -> 0 us
  waiting for transfers between devices: 17.5 us -> 0 us
  other arithmetic: 4.41 us -> 0 us
  local copies, waits for them, and re-layouts: 2.45 us -> 5.17 us
  matrix products: 1.9 us -> 0 us
    pallas_call x0 -> x2, Pallas kernels: none -> 33.6 us  [the longest x1 30.8 us: local(): pl.pallas_call(gather_kernel, out_shape=(jax.ShapeDtypeStruct((N_FRAMES,...]
    all_to_all x1 -> x0, blocking collectives: 21 us -> none  [local(): lax.all_to_all(turned, 'chan', split_axis=2, concat_axis=3, tiled=True)]
    all_to_all x1 -> x0, waiting for transfers between devices: 16.6 us -> none  [from_everyone(): return lax.all_to_all(copies, axis, split_axis=0, concat_axis=0, tiled=True)]
    all_to_all x1 -> x0, starting transfers between devices: 13.2 us -> none  [from_everyone(): return lax.all_to_all(copies, axis, split_axis=0, concat_axis=0, tiled=True)]
    ppermute x3 -> x0, starting transfers between devices: 9.62 us -> none  [shifted(): return lax.ppermute(value, axis, pairs)]
    unnamed x8 -> x12, local copies, waits for them, and re-layouts: 0.02 us -> 5.17 us
    mul x2 -> x0, other arithmetic: 2.42 us -> none  [the longest x1 1.8 us: dft_table(): jnp.cos(angles) * scale]
    dot_general x2 -> x0, matrix products: 1.9 us -> none  [the longest x1 1.17 us: local(): jnp.einsum('kcp,fpi->kfci', tables, samples.astype(jnp.float32), precisio...]
  transfers between devices with their start and end apart: 4 -> 0, of which waited for: 2 -> 0; matrix products, arithmetic and copies ran while one was open for 0% -> 0% of each run, Pallas kernels for 0% -> 0%
where the time goes in v1:
time: 39.1 us; the launch traced here: 38.8 us
  Pallas kernels  33.6 us (86%)
  local copies, waits for them, and re-layouts  5.17 us (13%)
    pallas_call x1, Pallas kernels, local(): pl.pallas_call(gather_kernel, out_shape=(jax.ShapeDtypeStruct((N_FRAMES,...  30.8 us
    unnamed x12, local copies, waits for them, and re-layouts  5.17 us
    pallas_call x1, Pallas kernels, local(): pl.pallas_call(correlate_kernel, grid=(4,), out_shape=jax.ShapeDtypeStruc...  2.76 us

profile of v1, /device:TPU:1, one launch (start us, length us, event | category | flops | bytes accessed | tf_op | source)
XLA Modules:
  0.0 38.8 jit_solution(14488602725298488314)
XLA Ops:
  0.0 0.0 copy-start
  0.0 1.6 %copy-done = bf16[1,4096,256]{2,1,0:T(8,128)(2,1)S(1)} copy-done((bf16[1,4096,256]{2,1,0:T(8,128)(2,1)S(1)}, bf16[1,4096,256]{2,1,0:T(8,128)(2,1)}, u32[]{:S(2)}) %copy-start) | copy-done | bytes 2097176
  1.6 0.0 copy-start.1
  1.6 0.8 %copy-done.1 = f32[4,4096]{1,0:T(4,128)S(1)} copy-done((f32[4,4096]{1,0:T(4,128)S(1)}, f32[4,4096]{1,0:T(4,128)}, u32[]{:S(2)}) %copy-start.1) | copy-done | bytes 65560
  2.4 0.0 copy-start.2
  2.4 0.7 %copy-done.2 = f32[16,256]{1,0:T(8,128)S(1)} copy-done((f32[16,256]{1,0:T(8,128)S(1)}, f32[16,256]{1,0:T(8,128)}, u32[]{:S(2)}) %copy-start.2) | copy-done | bytes 16408
  3.1 0.0 copy-start.3
  3.2 0.7 %copy-done.3 = f32[16,256]{1,0:T(8,128)S(1)} copy-done((f32[16,256]{1,0:T(8,128)S(1)}, f32[16,256]{1,0:T(8,128)}, u32[]{:S(2)}) %copy-start.3) | copy-done | bytes 16408
  3.9 0.0 copy-start.4
  3.9 0.7 %copy-done.4 = s32[16]{0:T(128)S(1)} copy-done((s32[16]{0:T(128)S(1)}, s32[16]{0:T(128)}, u32[]{:S(2)}) %copy-start.4) | copy-done | bytes 88
  4.5 0.0 copy-start.5
  4.5 0.7 %copy-done.5 = s32[128]{0:T(128)S(1)} copy-done((s32[128]{0:T(128)S(1)}, s32[128]{0:T(128)}, u32[]{:S(2)}) %copy-start.5) | copy-done | bytes 536
  5.2 30.8 %spectra_and_gather.1 = (bf16[32,4,2,256]{3,2,1,0:T(2,128)(2,1)S(1)}, bf16[32,2,2,256]{3,2,1,0:T(2,128)(2,1)S(1)}) custom-call(bf16[1,4096,256]{2,1,0:T(8,128)(2,1)S(1)} %copy-done, s32[16]{0:T(128)S(1)} %copy-done.4, f32[4,4096]{1,0:T(4,128)S(1)} %copy-done.1, f32[16,256]{1,0:T(8,128)S(1)} %copy-done.2, f32[16,256]{1,0:T(8,128)S(1)} %copy-done.3, ...), custom_call_target="tpu_custom_call" | custom-call | tf_op jit(solution)/shard_map/spectra_and_gather/pallas_call | solution.py:267
  36.0 2.8 %correlate.1 = bf16[2,1,1024,512]{3,2,1,0:T(8,128)(2,1)} custom-call(bf16[32,4,2,256]{3,2,1,0:T(2,128)(2,1)S(1)} %get-tuple-element.7.rows, bf16[32,2,2,256]{3,2,1,0:T(2,128)(2,1)S(1)} %get-tuple-element.8.cols), custom_call_target="tpu_custom_call" | custom-call | tf_op jit(solution)/shard_map/correlate/pallas_call | solution.py:299
Async XLA Ops:
  0.0 1.6 %copy-start = (bf16[1,4096,256]{2,1,0:T(8,128)(2,1)S(1)}, bf16[1,4096,256]{2,1,0:T(8,128)(2,1)}, u32[]{:S(2)}) copy-start(bf16[1,4096,256]{2,1,0:T(8,128)(2,1)} %x_hbm.1) | copy-start | bytes 6291460
  1.6 0.8 %copy-start.1 = (f32[4,4096]{1,0:T(4,128)S(1)}, f32[4,4096]{1,0:T(4,128)}, u32[]{:S(2)}) copy-start(f32[4,4096]{1,0:T(4,128)} %constant.2.clone.filt_hbm) | copy-start | bytes 196612
  2.4 0.7 %copy-start.2 = (f32[16,256]{1,0:T(8,128)S(1)}, f32[16,256]{1,0:T(8,128)}, u32[]{:S(2)}) copy-start(f32[16,256]{1,0:T(8,128)} %gr_hbm.1) | copy-start | bytes 49156
  3.1 0.7 %copy-start.3 = (f32[16,256]{1,0:T(8,128)S(1)}, f32[16,256]{1,0:T(8,128)}, u32[]{:S(2)}) copy-start(f32[16,256]{1,0:T(8,128)} %gi_hbm.1) | copy-start | bytes 49156
  3.9 0.7 %copy-start.4 = (s32[16]{0:T(128)S(1)}, s32[16]{0:T(128)}, u32[]{:S(2)}) copy-start(s32[16]{0:T(128)} %ci_hbm.1) | copy-start | bytes 196
  4.5 0.7 %copy-start.5 = (s32[128]{0:T(128)S(1)}, s32[128]{0:T(128)}, u32[]{:S(2)}) copy-start(s32[128]{0:T(128)} %param.10) | copy-start | bytes 1540

commit v2 on v1

--- a/solution.py
+++ b/solution.py
@@ -262,7 +262,7 @@
 
 
 def local(samples, channel_index, gain_real, gain_imag, flags):
-    anywhere = pl.BlockSpec(memory_space=pl.ANY)
+    in_hbm = pl.BlockSpec(memory_space=pltpu.HBM)
     vmem = pl.BlockSpec(memory_space=pltpu.VMEM)
     rows, cols = pl.pallas_call(
         gather_kernel,
@@ -270,7 +270,7 @@
             jax.ShapeDtypeStruct((N_FRAMES, 4, 2, BLOCK), BF16),
             jax.ShapeDtypeStruct((N_FRAMES, 2, 2, BLOCK), BF16),
         ),
-        in_specs=[anywhere] * 6,
+        in_specs=[in_hbm] * 6,
         out_specs=(vmem, vmem),
         scratch_shapes=[
             pltpu.VMEM((P_SIZE, BLOCK), BF16),
@@ -294,8 +294,11 @@
             collective_id=0, has_side_effects=True, vmem_limit_bytes=16 * 2**20
         ),
         name="spectra_and_gather",
-    )(samples, channel_index, jnp.asarray(filter_taps()), gain_real, gain_imag,
-      flags.reshape(1, 128))
+    )(*[
+        pltpu.with_memory_space_constraint(value, pltpu.HBM)
+        for value in (samples, channel_index, jnp.asarray(filter_taps()), gain_real, gain_imag,
+                      flags.reshape(1, 128))
+    ])
     return pl.pallas_call(
         correlate_kernel,
         grid=(4,),

time: 39.1 us -> 33.4 us (0.85)
  local copies, waits for them, and re-layouts: 5.17 us -> 0 us
    unnamed x12 -> x0, local copies, waits for them, and re-layouts: 5.17 us -> none
where the time goes in v2:
time: 33.4 us; the launch traced here: 33.3 us
  Pallas kernels  33.3 us (100%)
    pallas_call x1, Pallas kernels, local(): pl.pallas_call(gather_kernel, out_shape=(jax.ShapeDtypeStruct((N_FRAMES,...  30.6 us
    pallas_call x1, Pallas kernels, local(): pl.pallas_call(correlate_kernel, grid=(4,), out_shape=jax.ShapeDtypeStruc...  2.77 us

profile of v2, /device:TPU:1, one launch (start us, length us, event | category | flops | bytes accessed | tf_op | source)
XLA Modules:
  0.0 33.3 jit_solution(17378577599755082700)
XLA Ops:
  0.0 30.6 %spectra_and_gather.1 = (bf16[32,4,2,256]{3,2,1,0:T(2,128)(2,1)S(1)}, bf16[32,2,2,256]{3,2,1,0:T(2,128)(2,1)S(1)}) custom-call(bf16[1,4096,256]{2,1,0:T(8,128)(2,1)} %x_hbm.1, s32[16]{0:T(128)} %ci_hbm.1, f32[4,4096]{1,0:T(4,128)} %constant.2.clone.filt_hbm, f32[16,256]{1,0:T(8,128)} %gr_hbm.1, f32[16,256]{1,0:T(8,128)} %gi_hbm.1, s32[1,128]{1,0:T(1,128)} %bitcast.1), custom_call_target="tpu_custom_call" | custom-call | tf_op jit(solution)/shard_map/spectra_and_gather/pallas_call | solution.py:267
  30.6 2.8 %correlate.1 = bf16[2,1,1024,512]{3,2,1,0:T(8,128)(2,1)} custom-call(bf16[32,4,2,256]{3,2,1,0:T(2,128)(2,1)S(1)} %get-tuple-element.7.rows, bf16[32,2,2,256]{3,2,1,0:T(2,128)(2,1)S(1)} %get-tuple-element.8.cols), custom_call_target="tpu_custom_call" | custom-call | tf_op jit(solution)/shard_map/correlate/pallas_call | solution.py:302

commit v3 on v2

--- a/solution.py
+++ b/solution.py
@@ -42,9 +42,7 @@
     return cos, sin
 
 
-def far_first(i):
-    half = (i + 1) // 2
-    return 4 + half * (1 - 2 * (i % 2))
+FAR_FIRST = (4, 3, 5, 2, 6, 1, 7, 0)
 
 
 def gather_kernel(
@@ -57,6 +55,31 @@
     me_t = lax.axis_index("tm")
     me_r = lax.axis_index("row")
     frame = me_t * N_ROW + me_r
+    z_at = [lax.rem(lax.rem(me_c, 8) + step, 8) for step in FAR_FIRST]
+    half_at = [lax.rem(lax.div(me_c, 8) + step, 2) * 8 for step in (1, 0)]
+    chans = [half + z for z in z_at for half in half_at]
+    tms = [lax.rem(me_t + step, N_TM) for step in FAR_FIRST]
+    rows_at = [lax.rem(me_r + step, N_ROW) for step in (2, 3, 1, 0)]
+    group = [(t, r) for t in tms for r in rows_at][:-1]
+
+    def place(number):
+        return lax.div(number, N_ROW), lax.rem(number, N_ROW)
+
+    barrier = pltpu.get_barrier_semaphore()
+
+    def greet(c, t, r):
+        pl.semaphore_signal(barrier, inc=1, device_id=(c, t, r), device_id_type=MESH)
+
+    for back in range(TAPS - 1, 0, -1):
+        @pl.when(frame >= back)
+        def _():
+            for c in chans[:-1]:
+                greet(c, *place(frame - back))
+
+    for c in chans[:-1]:
+        greet(c, me_t, me_r)
+    for t, r in group:
+        greet(me_c, t, r)
 
     loads = [
         pltpu.make_async_copy(src, dst, local_sems.at[i])
@@ -67,32 +90,6 @@
     ]
     for copy in loads:
         copy.start()
-
-    barrier = pltpu.get_barrier_semaphore()
-
-    def greet_chan(i, _):
-        peer = (me_c + i) % N_CHAN
-        for back in range(TAPS):
-            @pl.when(frame >= back)
-            def _():
-                other = frame - back
-                pl.semaphore_signal(
-                    barrier, inc=1,
-                    device_id=(peer, other // N_ROW, other % N_ROW), device_id_type=MESH,
-                )
-        return 0
-
-    lax.fori_loop(1, N_CHAN, greet_chan, 0)
-
-    def greet_frames(i, _):
-        other = (frame + i) % N_FRAMES
-        pl.semaphore_signal(
-            barrier, inc=1,
-            device_id=(me_c, other // N_ROW, other % N_ROW), device_id_type=MESH,
-        )
-        return 0
-
-    lax.fori_loop(1, N_FRAMES, greet_frames, 0)
 
     for before in range(1, TAPS):
         @pl.when(frame < before)
@@ -158,34 +155,26 @@
     ahead_count = jnp.minimum(N_FRAMES - 1 - frame, TAPS - 1)
     pl.semaphore_wait(barrier, (N_CHAN - 1) * (1 + ahead_count) + N_FRAMES - 1)
 
-    def part_copy(c, ahead):
+    def send_part(c, ahead):
         k = TAPS - 1 - ahead
-        other = frame + ahead
-        return pltpu.make_async_remote_copy(
+        pltpu.make_async_remote_copy(
             src_ref=send.at[c * TAPS + k],
             dst_ref=parts.at[k, me_c],
             send_sem=send_sem1.at[k],
             recv_sem=parts_sems.at[k],
-            device_id=(c, other // N_ROW, other % N_ROW),
+            device_id=(c, *place(frame + ahead)),
             device_id_type=MESH,
-        )
-
-    def send_parts(i, _):
-        z = (me_c % 8 + far_first(i % 8)) % 8
-        half = (me_c // 8 + 1 + i // 8) % 2
-        c = half * 8 + z
-        for ahead in range(TAPS - 1, 0, -1):
-            @pl.when(frame + ahead < N_FRAMES)
-            def _():
-                part_copy(c, ahead).start()
-
-        @pl.when(i < N_CHAN - 1)
-        def _():
-            part_copy(c, 0).start()
-        return 0
-
+        ).start()
+
+    for ahead in range(TAPS - 1, 0, -1):
+        @pl.when(frame + ahead < N_FRAMES)
+        def _():
+            for c in chans:
+                send_part(c, ahead)
+
+    for c in chans[:-1]:
+        send_part(c, 0)
     parts[TAPS - 1, me_c] = send[me_c * TAPS + TAPS - 1]
-    lax.fori_loop(0, N_CHAN, send_parts, 0)
 
     for k in range(TAPS - 1):
         @pl.when(frame >= TAPS - 1 - k)
@@ -196,36 +185,21 @@
 
     volts[...] = (((parts[0] + parts[1]) + parts[2]) + parts[3]).astype(BF16)
 
-    def volt_copies(t, r):
-        rows = pltpu.make_async_remote_copy(
-            src_ref=volts.at[pl.ds(r * 4, 4)],
-            dst_ref=rows_out.at[frame],
-            send_sem=send_sem2.at[0],
-            recv_sem=rows_sem,
-            device_id=(me_c, t, r),
-            device_id_type=MESH,
-        )
-        cols = pltpu.make_async_remote_copy(
-            src_ref=volts.at[pl.ds(t * 2, 2)],
-            dst_ref=cols_out.at[frame],
-            send_sem=send_sem2.at[1],
-            recv_sem=cols_sem,
-            device_id=(me_c, t, r),
-            device_id_type=MESH,
-        )
-        return rows, cols
-
-    def send_volts(i, _):
-        t = (me_t + far_first(i // 4)) % N_TM
-        r = (me_r + 1 + i % 4) % N_ROW
-        rows, cols = volt_copies(t, r)
-        rows.start()
-        cols.start()
-        return 0
-
+    for t, r in group:
+        for src, dst, at, sem in (
+            (volts.at[pl.ds(r * 4, 4)], rows_out, 0, rows_sem),
+            (volts.at[pl.ds(t * 2, 2)], cols_out, 1, cols_sem),
+        ):
+            pltpu.make_async_remote_copy(
+                src_ref=src,
+                dst_ref=dst.at[frame],
+                send_sem=send_sem2.at[at],
+                recv_sem=sem,
+                device_id=(me_c, t, r),
+                device_id_type=MESH,
+            ).start()
     rows_out[frame] = volts[pl.ds(me_r * 4, 4)]
     cols_out[frame] = volts[pl.ds(me_t * 2, 2)]
-    lax.fori_loop(0, N_FRAMES - 1, send_volts, 0)
 
     for ref, sem in ((rows_out, rows_sem), (cols_out, cols_sem)):
         others = ref.at[pl.ds(0, N_FRAMES - 1)]

time: 33.4 us -> 32.9 us (0.985)
  Pallas kernels: 33.3 us -> 32.7 us
    pallas_call x1, Pallas kernels: 30.6 us -> 30 us  [local(): pl.pallas_call(gather_kernel, out_shape=(jax.ShapeDtypeStruct((N_FRAMES,...]
where the time goes in v3:
time: 32.9 us; the launch traced here: 32.8 us
  Pallas kernels  32.7 us (99%)
    pallas_call x1, Pallas kernels, local(): pl.pallas_call(gather_kernel, out_shape=(jax.ShapeDtypeStruct((N_FRAMES,...  30 us
    pallas_call x1, Pallas kernels, local(): pl.pallas_call(correlate_kernel, grid=(4,), out_shape=jax.ShapeDtypeStruc...  2.77 us

profile of v3, /device:TPU:1, one launch (start us, length us, event | category | flops | bytes accessed | tf_op | source)
XLA Modules:
  0.0 32.8 jit_solution(5978784269850908572)
XLA Ops:
  0.0 30.0 %spectra_and_gather.1 = (bf16[32,4,2,256]{3,2,1,0:T(2,128)(2,1)S(1)}, bf16[32,2,2,256]{3,2,1,0:T(2,128)(2,1)S(1)}) custom-call(bf16[1,4096,256]{2,1,0:T(8,128)(2,1)} %x_hbm.1, s32[16]{0:T(128)} %ci_hbm.1, f32[4,4096]{1,0:T(4,128)} %constant.2.clone.filt_hbm, f32[16,256]{1,0:T(8,128)} %gr_hbm.1, f32[16,256]{1,0:T(8,128)} %gi_hbm.1, s32[1,128]{1,0:T(1,128)} %bitcast.1), custom_call_target="tpu_custom_call" | custom-call | tf_op jit(solution)/shard_map/spectra_and_gather/pallas_call | solution.py:241
  30.0 2.8 %correlate.1 = bf16[2,1,1024,512]{3,2,1,0:T(8,128)(2,1)} custom-call(bf16[32,4,2,256]{3,2,1,0:T(2,128)(2,1)S(1)} %get-tuple-element.7.rows, bf16[32,2,2,256]{3,2,1,0:T(2,128)(2,1)S(1)} %get-tuple-element.8.cols), custom_call_target="tpu_custom_call" | custom-call | tf_op jit(solution)/shard_map/correlate/pallas_call | solution.py:276

commit v4 on v3

--- a/solution.py
+++ b/solution.py
@@ -16,6 +16,7 @@
 N_FRAMES = N_TM * N_ROW
 BLOCK = 256
 CHUNK = 512
+STRIP, STRIPS = 128, 8
 MESH = pl.DeviceIdType.MESH
 F32, BF16 = jnp.float32, jnp.bfloat16
 
@@ -166,14 +167,17 @@
             device_id_type=MESH,
         ).start()
 
-    for ahead in range(TAPS - 1, 0, -1):
-        @pl.when(frame + ahead < N_FRAMES)
-        def _():
-            for c in chans:
-                send_part(c, ahead)
-
-    for c in chans[:-1]:
-        send_part(c, 0)
+    for z in range(8):
+        for ahead in range(TAPS - 1, 0, -1):
+            @pl.when(frame + ahead < N_FRAMES)
+            def _():
+                for half in (0, 8):
+                    send_part(half + z, ahead)
+
+        for half in (0, 8):
+            @pl.when(me_c != half + z)
+            def _():
+                send_part(half + z, 0)
     parts[TAPS - 1, me_c] = send[me_c * TAPS + TAPS - 1]
 
     for k in range(TAPS - 1):
@@ -185,7 +189,7 @@
 
     volts[...] = (((parts[0] + parts[1]) + parts[2]) + parts[3]).astype(BF16)
 
-    for t, r in group:
+    def send_volts(t, r):
         for src, dst, at, sem in (
             (volts.at[pl.ds(r * 4, 4)], rows_out, 0, rows_sem),
             (volts.at[pl.ds(t * 2, 2)], cols_out, 1, cols_sem),
@@ -198,6 +202,13 @@
                 device_id=(me_c, t, r),
                 device_id_type=MESH,
             ).start()
+
+    for t in (0, 1, 7, 2, 6, 3, 5, 4):
+        for r in (1, 3, 2, 0):
+            @pl.when(frame != t * N_ROW + r)
+            def _():
+                send_volts(t, r)
+
     rows_out[frame] = volts[pl.ds(me_r * 4, 4)]
     cols_out[frame] = volts[pl.ds(me_t * 2, 2)]
 
@@ -215,24 +226,32 @@
         pltpu.make_async_copy(others, others, send_sem2.at[at]).wait()
 
 
-def correlate_kernel(rows, cols, out, right):
-    @pl.when(pl.program_id(0) == 0)
-    def _():
-        to = lax.broadcasted_iota(jnp.int32, (64, 64), 0)
-        at = lax.broadcasted_iota(jnp.int32, (64, 64), 1)
-        sign = jnp.where(to % 2 == 0, -1.0, 1.0)
-        swap = jnp.where(at == to + 1 - 2 * (to % 2), sign, 0.0).astype(BF16)
-        panel = jnp.concatenate([cols[:, 0].reshape(64, BLOCK), cols[:, 1].reshape(64, BLOCK)], 1)
-        right[:, :512] = panel
-        right[:, 512:] = jnp.dot(swap, panel, preferred_element_type=F32).astype(BF16)
-
-    left = rows[:, pl.program_id(0)].reshape(64, BLOCK)
-    product = lax.dot_general(
-        left, right[...], (((0,), (0,)), ((), ())), preferred_element_type=F32
-    )
-    product = product * (1.0 / N_FRAMES)
-    out[0, 0] = product[:, :512].astype(BF16)
-    out[1, 0] = product[:, 512:].astype(BF16)
+def correlate_kernel(rows, cols, out_hbm, right, out, sems):
+    to = lax.broadcasted_iota(jnp.int32, (64, 64), 0)
+    at = lax.broadcasted_iota(jnp.int32, (64, 64), 1)
+    sign = jnp.where(to % 2 == 0, -1.0, 1.0)
+    swap = jnp.where(at == to + 1 - 2 * (to % 2), sign, 0.0).astype(BF16)
+    panel = jnp.concatenate([cols[:, 0].reshape(64, BLOCK), cols[:, 1].reshape(64, BLOCK)], 1)
+    panel = panel * jnp.asarray(1.0 / N_FRAMES, BF16)
+    right[:, :512] = panel
+    right[:, 512:] = jnp.dot(swap, panel, preferred_element_type=F32).astype(BF16)
+
+    copies = []
+    for i in range(STRIPS):
+        left = rows[:, i // 2, :, (i % 2) * STRIP : (i % 2 + 1) * STRIP].reshape(64, STRIP)
+        product = lax.dot_general(
+            left, right[...], (((0,), (0,)), ((), ())), preferred_element_type=F32
+        )
+        out[i, 0] = product[:, :512].astype(BF16)
+        out[i, 1] = product[:, 512:].astype(BF16)
+        copies.append(
+            pltpu.make_async_copy(
+                out.at[i], out_hbm.at[:, 0, pl.ds(i * STRIP, STRIP), :], sems.at[i]
+            )
+        )
+        copies[-1].start()
+    for copy in copies:
+        copy.wait()
 
 
 def local(samples, channel_index, gain_real, gain_imag, flags):
@@ -275,11 +294,14 @@
     ])
     return pl.pallas_call(
         correlate_kernel,
-        grid=(4,),
         out_shape=jax.ShapeDtypeStruct((2, 1, 1024, 512), BF16),
         in_specs=[vmem, vmem],
-        out_specs=pl.BlockSpec((2, 1, BLOCK, 512), lambda i: (0, 0, i, 0)),
-        scratch_shapes=[pltpu.VMEM((64, 1024), BF16)],
+        out_specs=pl.BlockSpec(memory_space=pltpu.HBM),
+        scratch_shapes=[
+            pltpu.VMEM((64, 1024), BF16),
+            pltpu.VMEM((STRIPS, 2, STRIP, 512), BF16),
+            pltpu.SemaphoreType.DMA((STRIPS,)),
+        ],
         compiler_params=pltpu.CompilerParams(vmem_limit_bytes=16 * 2**20),
         name="correlate",
     )(rows, cols)

time: 32.9 us -> 31 us (0.942)
  Pallas kernels: 32.7 us -> 30.8 us
    pallas_call x1, Pallas kernels: 2.77 us -> 1.71 us  [local(): pl.pallas_call(correlate_kernel, out_shape=jax.ShapeDtypeStruct((2, 1, 10...]
    pallas_call x1, Pallas kernels: 30 us -> 29.1 us  [local(): pl.pallas_call(gather_kernel, out_shape=(jax.ShapeDtypeStruct((N_FRAMES,...]
where the time goes in v4:
time: 31 us; the launch traced here: 30.9 us
  Pallas kernels  30.8 us (99%)
    pallas_call x1, Pallas kernels, local(): pl.pallas_call(gather_kernel, out_shape=(jax.ShapeDtypeStruct((N_FRAMES,...  29.1 us
    pallas_call x1, Pallas kernels, local(): pl.pallas_call(correlate_kernel, out_shape=jax.ShapeDtypeStruct((2, 1, 10...  1.71 us

profile of v4, /device:TPU:1, one launch (start us, length us, event | category | flops | bytes accessed | tf_op | source)
XLA Modules:
  0.0 30.9 jit_solution(3477307846962331118)
XLA Ops:
  0.0 29.1 %spectra_and_gather.1 = (bf16[32,4,2,256]{3,2,1,0:T(2,128)(2,1)S(1)}, bf16[32,2,2,256]{3,2,1,0:T(2,128)(2,1)S(1)}) custom-call(bf16[1,4096,256]{2,1,0:T(8,128)(2,1)} %x_hbm.1, s32[16]{0:T(128)} %ci_hbm.1, f32[4,4096]{1,0:T(4,128)} %constant.2.clone.filt_hbm, f32[16,256]{1,0:T(8,128)} %gr_hbm.1, f32[16,256]{1,0:T(8,128)} %gi_hbm.1, s32[1,128]{1,0:T(1,128)} %bitcast.1), custom_call_target="tpu_custom_call" | custom-call | tf_op jit(solution)/shard_map/spectra_and_gather/pallas_call | solution.py:260
  29.1 1.7 %correlate.1 = bf16[2,1,1024,512]{3,2,1,0:T(8,128)(2,1)} custom-call(bf16[32,4,2,256]{3,2,1,0:T(2,128)(2,1)S(1)} %get-tuple-element.7.rows, bf16[32,2,2,256]{3,2,1,0:T(2,128)(2,1)S(1)} %get-tuple-element.8.cols), custom_call_target="tpu_custom_call" | custom-call | tf_op jit(solution)/shard_map/correlate/pallas_call | solution.py:295

commit v5 on v4

--- a/solution.py
+++ b/solution.py
@@ -50,37 +50,47 @@
     x_hbm, ci_hbm, filt_hbm, gr_hbm, gi_hbm, flags_hbm,
     rows_out, cols_out,
     x, ci, filt, gr, gi, flags, lhs, send, parts, volts,
-    local_sems, send_sem1, send_sem2, parts_sems, rows_sem, cols_sem,
+    local_sems, send_sem1, send_sem2, parts_sems, volts_sems,
 ):
     me_c = lax.axis_index("chan")
     me_t = lax.axis_index("tm")
     me_r = lax.axis_index("row")
     frame = me_t * N_ROW + me_r
-    z_at = [lax.rem(lax.rem(me_c, 8) + step, 8) for step in FAR_FIRST]
-    half_at = [lax.rem(lax.div(me_c, 8) + step, 2) * 8 for step in (1, 0)]
-    chans = [half + z for z in z_at for half in half_at]
-    tms = [lax.rem(me_t + step, N_TM) for step in FAR_FIRST]
-    rows_at = [lax.rem(me_r + step, N_ROW) for step in (2, 3, 1, 0)]
-    group = [(t, r) for t in tms for r in rows_at][:-1]
+    me_z = lax.rem(me_c, 8)
+    me_half = lax.div(me_c, 8)
+    rows_half = lax.div(me_r, 2)
+    cols_half = lax.div(me_t, 4)
+    ahead_count = jnp.minimum(N_FRAMES - 1 - frame, TAPS - 1)
+    rows_count = N_FRAMES - jnp.where(rows_half == me_half, 1, 0)
+    cols_count = N_FRAMES - jnp.where(cols_half == me_half, 1, 0)
 
     def place(number):
         return lax.div(number, N_ROW), lax.rem(number, N_ROW)
 
     barrier = pltpu.get_barrier_semaphore()
 
-    def greet(c, t, r):
-        pl.semaphore_signal(barrier, inc=1, device_id=(c, t, r), device_id_type=MESH)
-
+    def greet(c, at):
+        pl.semaphore_signal(barrier, inc=1, device_id=(c, *at), device_id_type=MESH)
+
+    line = [me_half * 8 + lax.rem(me_z + step, 8) for step in FAR_FIRST]
     for back in range(TAPS - 1, 0, -1):
         @pl.when(frame >= back)
         def _():
-            for c in chans[:-1]:
-                greet(c, *place(frame - back))
-
-    for c in chans[:-1]:
-        greet(c, me_t, me_r)
-    for t, r in group:
-        greet(me_c, t, r)
+            for c in line:
+                greet(c, place(frame - back))
+
+    for c in line[:-1]:
+        greet(c, (me_t, me_r))
+    rows_from = rows_half * 8 + me_z
+    cols_from = cols_half * 8 + me_z
+    for step in sorted(range(1, N_FRAMES), key=lambda j: abs(j - N_FRAMES // 2)):
+        at = place(lax.rem(frame + step, N_FRAMES))
+        greet(rows_from, at)
+        greet(cols_from, at)
+    for source in (rows_from, cols_from):
+        @pl.when(source != me_c)
+        def _():
+            greet(source, (me_t, me_r))
 
     loads = [
         pltpu.make_async_copy(src, dst, local_sems.at[i])
@@ -146,24 +156,23 @@
         planes += [real_gain * s_re - imag_gain * s_im, real_gain * s_im + imag_gain * s_re]
     planes = jnp.concatenate(planes, 0)
     to = lax.broadcasted_iota(jnp.int32, (128, 128), 0)
-    source = (to % 8) * 16 + to // 8
+    source = ((to // 4 % 4) * 2 + to % 2) * 16 + (to // 2 % 2) * 8 + to // 16
     turn = (lax.broadcasted_iota(jnp.int32, (128, 128), 1) == source).astype(F32)
     turned = jnp.dot(
         turn, planes, precision=lax.Precision.HIGHEST, preferred_element_type=F32
     )
-    send[...] = turned.reshape(64, 2, BLOCK)
-
-    ahead_count = jnp.minimum(N_FRAMES - 1 - frame, TAPS - 1)
-    pl.semaphore_wait(barrier, (N_CHAN - 1) * (1 + ahead_count) + N_FRAMES - 1)
-
-    def send_part(c, ahead):
+    send[...] = turned.reshape(32, 2, 2, BLOCK)
+
+    pl.semaphore_wait(barrier, 8 * (1 + ahead_count) - 1 + rows_count + cols_count)
+
+    def send_part(z, ahead):
         k = TAPS - 1 - ahead
         pltpu.make_async_remote_copy(
-            src_ref=send.at[c * TAPS + k],
-            dst_ref=parts.at[k, me_c],
+            src_ref=send.at[z * TAPS + k],
+            dst_ref=parts.at[k, me_z],
             send_sem=send_sem1.at[k],
             recv_sem=parts_sems.at[k],
-            device_id=(c, *place(frame + ahead)),
+            device_id=(me_half * 8 + z, *place(frame + ahead)),
             device_id_type=MESH,
         ).start()
 
@@ -171,59 +180,77 @@
         for ahead in range(TAPS - 1, 0, -1):
             @pl.when(frame + ahead < N_FRAMES)
             def _():
-                for half in (0, 8):
-                    send_part(half + z, ahead)
-
-        for half in (0, 8):
-            @pl.when(me_c != half + z)
-            def _():
-                send_part(half + z, 0)
-    parts[TAPS - 1, me_c] = send[me_c * TAPS + TAPS - 1]
+                send_part(z, ahead)
+
+        @pl.when(me_z != z)
+        def _():
+            send_part(z, 0)
+    parts[TAPS - 1, me_z] = send[me_z * TAPS + TAPS - 1]
+
+    def wait_bytes(ref, sem):
+        pltpu.make_async_copy(ref, ref, sem).wait()
 
     for k in range(TAPS - 1):
         @pl.when(frame >= TAPS - 1 - k)
         def _():
-            pltpu.make_async_copy(parts.at[k], parts.at[k], parts_sems.at[k]).wait()
-    own = parts.at[TAPS - 1, pl.ds(0, N_CHAN - 1)]
-    pltpu.make_async_copy(own, own, parts_sems.at[TAPS - 1]).wait()
-
-    volts[...] = (((parts[0] + parts[1]) + parts[2]) + parts[3]).astype(BF16)
-
-    def send_volts(t, r):
-        for src, dst, at, sem in (
-            (volts.at[pl.ds(r * 4, 4)], rows_out, 0, rows_sem),
-            (volts.at[pl.ds(t * 2, 2)], cols_out, 1, cols_sem),
-        ):
+            wait_bytes(parts.at[k], parts_sems.at[k])
+    wait_bytes(parts.at[TAPS - 1, pl.ds(0, 7)], parts_sems.at[TAPS - 1])
+
+    for half in range(2):
+        total = parts[0, :, half] + parts[1, :, half] + parts[2, :, half] + parts[3, :, half]
+        volts[half] = total.astype(BF16)
+
+    def send_volts(half, first, count, out, at, t, r):
+        @pl.when((me_c != half * 8 + me_z) | (frame != t * N_ROW + r))
+        def _():
             pltpu.make_async_remote_copy(
-                src_ref=src,
-                dst_ref=dst.at[frame],
+                src_ref=volts.at[half, pl.ds(first, count)],
+                dst_ref=out.at[frame],
                 send_sem=send_sem2.at[at],
-                recv_sem=sem,
-                device_id=(me_c, t, r),
+                recv_sem=volts_sems.at[at],
+                device_id=(half * 8 + me_z, t, r),
                 device_id_type=MESH,
             ).start()
 
-    for t in (0, 1, 7, 2, 6, 3, 5, 4):
-        for r in (1, 3, 2, 0):
-            @pl.when(frame != t * N_ROW + r)
+    def send_rows(t):
+        for half in range(2):
+            for r in (1, 0):
+                send_volts(half, 4 * r, 4, rows_out, 0, t, me_half * 2 + r)
+
+    def send_cols(n):
+        part = n + me_half * (3 - 2 * n)
+        for half in range(2):
+            for r in (1, 3, 2, 0):
+                send_volts(half, 2 * part, 2, cols_out, 1, me_half * 4 + part, r)
+
+    for n, t in enumerate((0, 1, 2, 7, 3, 6, 5, 4)):
+        send_rows(t)
+        if n == 1:
+            for i in range(4):
+                send_cols(i)
+
+    @pl.when(rows_half == me_half)
+    def _():
+        rows_out[frame] = volts[me_half, pl.ds(4 * lax.rem(me_r, 2), 4)]
+
+    @pl.when(cols_half == me_half)
+    def _():
+        cols_out[frame] = volts[me_half, pl.ds(2 * lax.rem(me_t, 4), 2)]
+
+    for at, (ref, half) in enumerate(((rows_out, rows_half), (cols_out, cols_half))):
+        for sems in (volts_sems, send_sem2):
+            @pl.when(half == me_half)
             def _():
-                send_volts(t, r)
-
-    rows_out[frame] = volts[pl.ds(me_r * 4, 4)]
-    cols_out[frame] = volts[pl.ds(me_t * 2, 2)]
-
-    for ref, sem in ((rows_out, rows_sem), (cols_out, cols_sem)):
-        others = ref.at[pl.ds(0, N_FRAMES - 1)]
-        pltpu.make_async_copy(others, others, sem).wait()
-
+                wait_bytes(ref.at[pl.ds(0, N_FRAMES - 1)], sems.at[at])
+
+            @pl.when(half != me_half)
+            def _():
+                wait_bytes(ref, sems.at[at])
     for k in range(TAPS - 1):
         @pl.when(frame + TAPS - 1 - k < N_FRAMES)
         def _():
-            pltpu.make_async_copy(parts.at[k], parts.at[k], send_sem1.at[k]).wait()
-    pltpu.make_async_copy(own, own, send_sem1.at[TAPS - 1]).wait()
-    for ref, at in ((rows_out, 0), (cols_out, 1)):
-        others = ref.at[pl.ds(0, N_FRAMES - 1)]
-        pltpu.make_async_copy(others, others, send_sem2.at[at]).wait()
+            wait_bytes(parts.at[k], send_sem1.at[k])
+    wait_bytes(parts.at[TAPS - 1, pl.ds(0, 7)], send_sem1.at[TAPS - 1])
 
 
 def correlate_kernel(rows, cols, out_hbm, right, out, sems):
@@ -273,15 +300,14 @@
             pltpu.VMEM((CHANNELS, BLOCK), F32),
             pltpu.VMEM((1, 128), jnp.int32),
             pltpu.VMEM((256, P_SIZE), BF16),
-            pltpu.VMEM((CHANNELS * TAPS, 2, BLOCK), F32),
-            pltpu.VMEM((TAPS, N_CHAN, 2, BLOCK), F32),
-            pltpu.VMEM((N_CHAN, 2, BLOCK), BF16),
+            pltpu.VMEM((8 * TAPS, 2, 2, BLOCK), F32),
+            pltpu.VMEM((TAPS, 8, 2, 2, BLOCK), F32),
+            pltpu.VMEM((2, 8, 2, BLOCK), BF16),
             pltpu.SemaphoreType.DMA((6,)),
             pltpu.SemaphoreType.DMA((TAPS,)),
             pltpu.SemaphoreType.DMA((2,)),
             pltpu.SemaphoreType.DMA((TAPS,)),
-            pltpu.SemaphoreType.DMA,
-            pltpu.SemaphoreType.DMA,
+            pltpu.SemaphoreType.DMA((2,)),
         ],
         compiler_params=pltpu.CompilerParams(
             collective_id=0, has_side_effects=True, vmem_limit_bytes=16 * 2**20

time: 31 us -> 30.5 us (0.984); the launches traced: 30.9 us -> 30 us
  Pallas kernels: 30.8 us -> 30 us
    pallas_call x1, Pallas kernels: 29.1 us -> 28.3 us  [local(): pl.pallas_call(gather_kernel, out_shape=(jax.ShapeDtypeStruct((N_FRAMES,...]
where the time goes in v5:
time: 30.5 us; the launch traced here: 30 us
  Pallas kernels  30 us (98%)
    pallas_call x1, Pallas kernels, local(): pl.pallas_call(gather_kernel, out_shape=(jax.ShapeDtypeStruct((N_FRAMES,...  28.3 us
    pallas_call x1, Pallas kernels, local(): pl.pallas_call(correlate_kernel, out_shape=jax.ShapeDtypeStruct((2, 1, 10...  1.7 us

profile of v5, /device:TPU:1, one launch (start us, length us, event | category | flops | bytes accessed | tf_op | source)
XLA Modules:
  0.0 30.0 jit_solution(13324404599301703087)
XLA Ops:
  0.0 28.3 %spectra_and_gather.1 = (bf16[32,4,2,256]{3,2,1,0:T(2,128)(2,1)S(1)}, bf16[32,2,2,256]{3,2,1,0:T(2,128)(2,1)S(1)}) custom-call(bf16[1,4096,256]{2,1,0:T(8,128)(2,1)} %x_hbm.1, s32[16]{0:T(128)} %ci_hbm.1, f32[4,4096]{1,0:T(4,128)} %constant.2.clone.filt_hbm, f32[16,256]{1,0:T(8,128)} %gr_hbm.1, f32[16,256]{1,0:T(8,128)} %gi_hbm.1, s32[1,128]{1,0:T(1,128)} %bitcast.1), custom_call_target="tpu_custom_call" | custom-call | tf_op jit(solution)/shard_map/spectra_and_gather/pallas_call | solution.py:287
  28.3 1.7 %correlate.1 = bf16[2,1,1024,512]{3,2,1,0:T(8,128)(2,1)} custom-call(bf16[32,4,2,256]{3,2,1,0:T(2,128)(2,1)S(1)} %get-tuple-element.7.rows, bf16[32,2,2,256]{3,2,1,0:T(2,128)(2,1)S(1)} %get-tuple-element.8.cols), custom_call_target="tpu_custom_call" | custom-call | tf_op jit(solution)/shard_map/correlate/pallas_call | solution.py:321

commit v6 on v5

--- a/solution.py
+++ b/solution.py
@@ -48,8 +48,8 @@
 
 def gather_kernel(
     x_hbm, ci_hbm, filt_hbm, gr_hbm, gi_hbm, flags_hbm,
-    rows_out, cols_out,
-    x, ci, filt, gr, gi, flags, lhs, send, parts, volts,
+    rows_out, right,
+    x, ci, filt, gr, gi, flags, lhs, send, parts, volts, cols,
     local_sems, send_sem1, send_sem2, parts_sems, volts_sems,
 ):
     me_c = lax.axis_index("chan")
@@ -73,14 +73,6 @@
         pl.semaphore_signal(barrier, inc=1, device_id=(c, *at), device_id_type=MESH)
 
     line = [me_half * 8 + lax.rem(me_z + step, 8) for step in FAR_FIRST]
-    for back in range(TAPS - 1, 0, -1):
-        @pl.when(frame >= back)
-        def _():
-            for c in line:
-                greet(c, place(frame - back))
-
-    for c in line[:-1]:
-        greet(c, (me_t, me_r))
     rows_from = rows_half * 8 + me_z
     cols_from = cols_half * 8 + me_z
     for step in sorted(range(1, N_FRAMES), key=lambda j: abs(j - N_FRAMES // 2)):
@@ -91,6 +83,15 @@
         @pl.when(source != me_c)
         def _():
             greet(source, (me_t, me_r))
+
+    for back in range(TAPS - 1, 0, -1):
+        @pl.when(frame >= back)
+        def _():
+            for c in line:
+                greet(c, place(frame - back))
+
+    for c in line[:-1]:
+        greet(c, (me_t, me_r))
 
     loads = [
         pltpu.make_async_copy(src, dst, local_sems.at[i])
@@ -221,13 +222,18 @@
         part = n + me_half * (3 - 2 * n)
         for half in range(2):
             for r in (1, 3, 2, 0):
-                send_volts(half, 2 * part, 2, cols_out, 1, me_half * 4 + part, r)
-
-    for n, t in enumerate((0, 1, 2, 7, 3, 6, 5, 4)):
+                send_volts(half, 2 * part, 2, cols, 1, me_half * 4 + part, r)
+
+    for t in (0, 1):
         send_rows(t)
-        if n == 1:
-            for i in range(4):
-                send_cols(i)
+    for n in range(4):
+        send_cols(n)
+    for step in FAR_FIRST:
+        t = lax.rem(me_t + step, N_TM)
+
+        @pl.when((t != 0) & (t != 1))
+        def _():
+            send_rows(t)
 
     @pl.when(rows_half == me_half)
     def _():
@@ -235,25 +241,18 @@
 
     @pl.when(cols_half == me_half)
     def _():
-        cols_out[frame] = volts[me_half, pl.ds(2 * lax.rem(me_t, 4), 2)]
-
-    for at, (ref, half) in enumerate(((rows_out, rows_half), (cols_out, cols_half))):
-        for sems in (volts_sems, send_sem2):
-            @pl.when(half == me_half)
-            def _():
-                wait_bytes(ref.at[pl.ds(0, N_FRAMES - 1)], sems.at[at])
-
-            @pl.when(half != me_half)
-            def _():
-                wait_bytes(ref, sems.at[at])
-    for k in range(TAPS - 1):
-        @pl.when(frame + TAPS - 1 - k < N_FRAMES)
-        def _():
-            wait_bytes(parts.at[k], send_sem1.at[k])
-    wait_bytes(parts.at[TAPS - 1, pl.ds(0, 7)], send_sem1.at[TAPS - 1])
-
-
-def correlate_kernel(rows, cols, out_hbm, right, out, sems):
+        cols[frame] = volts[me_half, pl.ds(2 * lax.rem(me_t, 4), 2)]
+
+    def wait_volts(ref, half, sem):
+        @pl.when(half == me_half)
+        def _():
+            wait_bytes(ref.at[pl.ds(0, N_FRAMES - 1)], sem)
+
+        @pl.when(half != me_half)
+        def _():
+            wait_bytes(ref, sem)
+
+    wait_volts(cols, cols_half, volts_sems.at[1])
     to = lax.broadcasted_iota(jnp.int32, (64, 64), 0)
     at = lax.broadcasted_iota(jnp.int32, (64, 64), 1)
     sign = jnp.where(to % 2 == 0, -1.0, 1.0)
@@ -263,6 +262,17 @@
     right[:, :512] = panel
     right[:, 512:] = jnp.dot(swap, panel, preferred_element_type=F32).astype(BF16)
 
+    wait_volts(rows_out, rows_half, volts_sems.at[0])
+    wait_volts(rows_out, rows_half, send_sem2.at[0])
+    wait_volts(cols, cols_half, send_sem2.at[1])
+    for k in range(TAPS - 1):
+        @pl.when(frame + TAPS - 1 - k < N_FRAMES)
+        def _():
+            wait_bytes(parts.at[k], send_sem1.at[k])
+    wait_bytes(parts.at[TAPS - 1, pl.ds(0, 7)], send_sem1.at[TAPS - 1])
+
+
+def correlate_kernel(rows, right, out_hbm, out, sems):
     copies = []
     for i in range(STRIPS):
         left = rows[:, i // 2, :, (i % 2) * STRIP : (i % 2 + 1) * STRIP].reshape(64, STRIP)
@@ -284,11 +294,11 @@
 def local(samples, channel_index, gain_real, gain_imag, flags):
     in_hbm = pl.BlockSpec(memory_space=pltpu.HBM)
     vmem = pl.BlockSpec(memory_space=pltpu.VMEM)
-    rows, cols = pl.pallas_call(
+    rows, right = pl.pallas_call(
         gather_kernel,
         out_shape=(
             jax.ShapeDtypeStruct((N_FRAMES, 4, 2, BLOCK), BF16),
-            jax.ShapeDtypeStruct((N_FRAMES, 2, 2, BLOCK), BF16),
+            jax.ShapeDtypeStruct((64, 1024), BF16),
         ),
         in_specs=[in_hbm] * 6,
         out_specs=(vmem, vmem),
@@ -303,6 +313,7 @@
             pltpu.VMEM((8 * TAPS, 2, 2, BLOCK), F32),
             pltpu.VMEM((TAPS, 8, 2, 2, BLOCK), F32),
             pltpu.VMEM((2, 8, 2, BLOCK), BF16),
+            pltpu.VMEM((N_FRAMES, 2, 2, BLOCK), BF16),
             pltpu.SemaphoreType.DMA((6,)),
             pltpu.SemaphoreType.DMA((TAPS,)),
             pltpu.SemaphoreType.DMA((2,)),
@@ -324,13 +335,12 @@
         in_specs=[vmem, vmem],
         out_specs=pl.BlockSpec(memory_space=pltpu.HBM),
         scratch_shapes=[
-            pltpu.VMEM((64, 1024), BF16),
             pltpu.VMEM((STRIPS, 2, STRIP, 512), BF16),
             pltpu.SemaphoreType.DMA((STRIPS,)),
         ],
         compiler_params=pltpu.CompilerParams(vmem_limit_bytes=16 * 2**20),
         name="correlate",
-    )(rows, cols)
+    )(rows, right)
 
 
 def solution(mesh):

time: 30.5 us -> 30.5 us (level); the launches traced: 30 us -> 30.4 us
    pallas_call x1, Pallas kernels: 28.3 us -> 28.7 us  [local(): pl.pallas_call(gather_kernel, out_shape=(jax.ShapeDtypeStruct((N_FRAMES,...]
where the time goes in v6:
time: 30.5 us; the launch traced here: 30.4 us
  Pallas kernels  30.3 us (99%)
    pallas_call x1, Pallas kernels, local(): pl.pallas_call(gather_kernel, out_shape=(jax.ShapeDtypeStruct((N_FRAMES,...  28.7 us
    pallas_call x1, Pallas kernels, local(): pl.pallas_call(correlate_kernel, out_shape=jax.ShapeDtypeStruct((2, 1, 10...  1.63 us

profile of v6, /device:TPU:1, one launch (start us, length us, event | category | flops | bytes accessed | tf_op | source)
XLA Modules:
  0.0 30.4 jit_solution(1456303470040409458)
XLA Ops:
  0.0 28.7 %spectra_and_gather.1 = (bf16[32,4,2,256]{3,2,1,0:T(2,128)(2,1)S(1)}, bf16[64,1024]{1,0:T(8,128)(2,1)S(1)}) custom-call(bf16[1,4096,256]{2,1,0:T(8,128)(2,1)} %x_hbm.1, s32[16]{0:T(128)} %ci_hbm.1, f32[4,4096]{1,0:T(4,128)} %constant.2.clone.filt_hbm, f32[16,256]{1,0:T(8,128)} %gr_hbm.1, f32[16,256]{1,0:T(8,128)} %gi_hbm.1, s32[1,128]{1,0:T(1,128)} %bitcast.1), custom_call_target="tpu_custom_call" | custom-call | tf_op jit(solution)/shard_map/spectra_and_gather/pallas_call | solution.py:297
  28.7 1.6 %correlate.1 = bf16[2,1,1024,512]{3,2,1,0:T(8,128)(2,1)} custom-call(bf16[32,4,2,256]{3,2,1,0:T(2,128)(2,1)S(1)} %get-tuple-element.7.rows, bf16[64,1024]{1,0:T(8,128)(2,1)S(1)} %get-tuple-element.8.right), custom_call_target="tpu_custom_call" | custom-call | tf_op jit(solution)/shard_map/correlate/pallas_call | solution.py:332

commit v7 on v6

--- a/solution.py
+++ b/solution.py
@@ -224,16 +224,11 @@
             for r in (1, 3, 2, 0):
                 send_volts(half, 2 * part, 2, cols, 1, me_half * 4 + part, r)
 
-    for t in (0, 1):
+    for n, t in enumerate((0, 1, 2, 7, 3, 6, 5, 4)):
         send_rows(t)
-    for n in range(4):
-        send_cols(n)
-    for step in FAR_FIRST:
-        t = lax.rem(me_t + step, N_TM)
-
-        @pl.when((t != 0) & (t != 1))
-        def _():
-            send_rows(t)
+        if n == 1:
+            for i in range(4):
+                send_cols(i)
 
     @pl.when(rows_half == me_half)
     def _():

time: 30.5 us -> 30.5 us (level)
  no operation moved by 1% of the time
where the time goes in v7:
time: 30.5 us; the launch traced here: 30.3 us
  Pallas kernels  30.3 us (99%)
    pallas_call x1, Pallas kernels, local(): pl.pallas_call(gather_kernel, out_shape=(jax.ShapeDtypeStruct((N_FRAMES,...  28.7 us
    pallas_call x1, Pallas kernels, local(): pl.pallas_call(correlate_kernel, out_shape=jax.ShapeDtypeStruct((2, 1, 10...  1.64 us

profile of v7, /device:TPU:1, one launch (start us, length us, event | category | flops | bytes accessed | tf_op | source)
XLA Modules:
  0.0 30.3 jit_solution(14426502403445224238)
XLA Ops:
  0.0 28.7 %spectra_and_gather.1 = (bf16[32,4,2,256]{3,2,1,0:T(2,128)(2,1)S(1)}, bf16[64,1024]{1,0:T(8,128)(2,1)S(1)}) custom-call(bf16[1,4096,256]{2,1,0:T(8,128)(2,1)} %x_hbm.1, s32[16]{0:T(128)} %ci_hbm.1, f32[4,4096]{1,0:T(4,128)} %constant.2.clone.filt_hbm, f32[16,256]{1,0:T(8,128)} %gr_hbm.1, f32[16,256]{1,0:T(8,128)} %gi_hbm.1, s32[1,128]{1,0:T(1,128)} %bitcast.1), custom_call_target="tpu_custom_call" | custom-call | tf_op jit(solution)/shard_map/spectra_and_gather/pallas_call | solution.py:292
  28.7 1.6 %correlate.1 = bf16[2,1,1024,512]{3,2,1,0:T(8,128)(2,1)} custom-call(bf16[32,4,2,256]{3,2,1,0:T(2,128)(2,1)S(1)} %get-tuple-element.7.rows, bf16[64,1024]{1,0:T(8,128)(2,1)S(1)} %get-tuple-element.8.right), custom_call_target="tpu_custom_call" | custom-call | tf_op jit(solution)/shard_map/correlate/pallas_call | solution.py:327
